TPU v7x, 256 devices: a whole 4x4x8 slice. The times are simulated.
256 devices in a mesh: band: 128 (over z, x_lo, y, core), sub: 2 (over x_hi).
Axes of the slice: x: 4 (x_hi: 2, x_lo: 2; x = x_hi * 2 + x_lo), y: 4, z: 8, core: 2. Of those that a mesh axis runs over, the one named last changes fastest.
Arguments:
- land_values: bfloat16 [64, 4194304], P(None, ('band', 'sub')), may hold values from -6 to 6
- area_weights: bfloat16 [32768, 128, 128], P(('band', 'sub')), may hold values from 0.0019989014 to 0.029907227
- land_mask: int32 [4194304], P(('band', 'sub')), may hold values 0 or 1
- dest_band: int32 [32768, 1], P(('band', 'sub')), may hold values from 0 to 127; in each aligned block of 128 rows (0 to 127, 128 to 255, ...) at most 2 rows name the same one
- dest_tile: int32 [32768], P(('band', 'sub')), may hold values from 0 to 399
- ocean_mask: int32 [6553600], P(('band', 'sub')), may hold values 0 or 1
Outputs:
- remapped: float32 [64, 6553600], P(None, ('band', 'sub'))
Inputs may be any that keep to these rules, and one draw needn't show every extreme that they name: `dest_band`: each device's 128 blocks name any one band at most 2 times; in every draw some device names one band exactly 2 times.
All inputs are finite; a program needn't handle non-finite values. No bound on the sum of `land_mask` or of `ocean_mask` on one device may be relied on, other than what follows from the above.
Results may differ from a plain program's by a relative error of at most 0.005.
Values may be sent and summed in bfloat16 or wider, within the bound.
A program may use at most 128 MiB of HBM per device.

v0:
```python
import jax
import jax.numpy as jnp
from jax import lax
from jax.sharding import PartitionSpec as P

cover_floor = 0.5


def cut_along(shard, dim, size):
    before, after = (shard.shape[:dim], shard.shape[dim + 1 :])
    return jnp.moveaxis(shard.reshape(*before, size, -1, *after), dim, 0)


def sent_and_summed(shard, axis, dim):
    size = lax.axis_size(axis)
    pieces = lax.all_to_all(cut_along(shard, dim, size), axis, 0, 0, tiled=True)
    return jnp.sum(pieces.astype(jnp.float32), axis=0)


def slot_table(group_key, slot_count, capacity):
    block_order = jnp.arange(group_key.shape[0], dtype=jnp.int32)
    earlier = (group_key[:, None] == group_key[None, :]) & (
        block_order[None, :] < block_order[:, None]
    )
    rank_in = jnp.sum(earlier.astype(jnp.int32), axis=1)
    slot_of = group_key * capacity + rank_in
    return jnp.arange(slot_count, dtype=jnp.int32)[:, None] == slot_of[None, :]


def place_tiles(partial_value, covered, tile_recv, tile_count):
    placing = (tile_recv[:, None] == jnp.arange(tile_count, dtype=jnp.int32)[None, :]).astype(
        jnp.bfloat16
    )
    summed = jnp.einsum("st,sfo->fto", placing, partial_value, preferred_element_type=jnp.float32)
    coverage = jnp.einsum("st,so->to", placing, covered, preferred_element_type=jnp.float32)
    return (summed, coverage)


def per_device(land_values, area_weights, land_mask, dest_band, dest_tile, ocean_mask):
    fields = land_values.shape[0]
    blocks_here = area_weights.shape[0]
    block_cells = area_weights.shape[1]
    tile_cells = area_weights.shape[2]
    band_count = lax.axis_size("band")
    halves = lax.axis_size("sub")
    capacity = max(2, 2 * blocks_here // band_count)
    slot_count = band_count * capacity
    tiles_half = ocean_mask.shape[0] // tile_cells
    tiles_band = tiles_half * halves
    values = land_values.reshape(fields, blocks_here, block_cells)
    masked = (
        area_weights * land_mask.reshape(blocks_here, block_cells).astype(jnp.bfloat16)[:, :, None]
    )
    target = dest_band[:, 0]
    ocean_keep = ocean_mask.reshape(tiles_half, tile_cells).astype(jnp.float32)
    packing = slot_table(target, slot_count, capacity)
    pack_half = packing.astype(jnp.bfloat16)
    tile_sent = jnp.sum(packing.astype(jnp.int32) * dest_tile[None, :], axis=1).reshape(
        band_count, capacity
    )
    partial_local = jnp.einsum(
        "fbl,blo->bfo", values, masked, preferred_element_type=jnp.float32
    ).astype(jnp.bfloat16)
    covered_local = jnp.sum(masked.astype(jnp.float32), axis=1).astype(jnp.bfloat16)
    sent_partial = jnp.einsum(
        "sb,bfo->sfo", pack_half, partial_local, preferred_element_type=jnp.float32
    ).astype(jnp.bfloat16)
    sent_partial = sent_partial.reshape(band_count, capacity, fields, tile_cells)
    sent_covered = jnp.einsum(
        "sb,bo->so", pack_half, covered_local, preferred_element_type=jnp.float32
    ).astype(jnp.bfloat16)
    sent_covered = sent_covered.reshape(band_count, capacity, tile_cells)
    partial_value, covered, tile_recv = (
        lax.all_to_all(sent_partial, "band", split_axis=0, concat_axis=0, tiled=True),
        lax.all_to_all(sent_covered, "band", split_axis=0, concat_axis=0, tiled=True),
        lax.all_to_all(tile_sent, "band", split_axis=0, concat_axis=0, tiled=True),
    )
    summed, coverage = place_tiles(
        partial_value.reshape(slot_count, fields, tile_cells),
        covered.reshape(slot_count, tile_cells),
        tile_recv.reshape(slot_count),
        tiles_band,
    )
    summed, coverage = (
        sent_and_summed(summed.astype(jnp.bfloat16), "sub", 1),
        sent_and_summed(coverage.astype(jnp.bfloat16), "sub", 0),
    )
    remapped = summed * ocean_keep[None] / jnp.maximum(coverage, cover_floor)[None]
    return remapped.reshape(fields, tiles_half * tile_cells)


def solution(mesh):
    in_specs = (
        P(None, ("band", "sub")),
        P(("band", "sub"), None, None),
        P(("band", "sub")),
        P(("band", "sub"), None),
        P(("band", "sub")),
        P(("band", "sub")),
    )
    out_specs = P(None, ("band", "sub"))
    return jax.shard_map(
        per_device, mesh=mesh, in_specs=in_specs, out_specs=out_specs, check_vma=False
    )
```

profile of v0, /device:TPU:17, one launch (start us, length us, event | category | flops | bytes accessed | tf_op | source)
XLA Modules:
  0.0 260.1 jit_solution(5637007530095761603)
XLA Ops:
  0.0 1.0 convert_reduce_fusion.2
  1.0 0.7 multiply_add_fusion
  1.7 0.8 select_reduce_fusion
  2.4 0.8 all_to_all.19
  3.2 14.0 %all-to-all-start.1 = ((s32[128,1,2]{2,1,0:T(1,128)}), s32[128,1,2]{2,1,0:T(1,128)S(1)}, u32[]{:S(2)}, u32[]{:S(2)}) async-start(s32[128,1,2]{2,1,0:T(1,128)} %bitcast.6), calls=%async_computation.1 | async-start | bytes 131072 | tf_op jit(solution)/shard_map/all_to_all | solution.py:76
  17.2 1.0 convert_bitcast_fusion.1
  18.2 4.7 %multiply_reduce_fusion = bf16[128,128]{1,0:T(8,128)(2,1)S(1)} fusion(bf16[128,128,128]{2,1,0:T(8,128)(2,1)} %param.7, bf16[128,128]{1,0:T(8,128)(2,1)S(1)} %convert_bitcast_fusion.1), kind=kLoop, calls=%fused_computation.5 | loop fusion | flops 4177920 | bytes 4259840 | tf_op jit(solution)/shard_map/reduce_sum | solution.py:64
  22.9 4.1 %convert_bitcast_fusion = bf16[128,64,128]{2,1,0:T(8,128)(2,1)} fusion(bf16[128,128,128]{2,1,0:T(8,128)(2,1)S(1)} %copy-done.1, bf16[128,128]{1,0:T(8,128)(2,1)S(1)} %convert_bitcast_fusion.1, bf16[64,16384]{1,0:T(8,128)(2,1)S(1)} %copy-done), kind=kOutput, calls=%fused_computation.12 | convolution fusion | flops 277872640 | bytes 8421376 | tf_op jit(solution)/shard_map/fbl,blo->bfo/dot_general | solution.py:61
  27.0 0.8 convolution_convert_fusion.3
  27.8 12.3 %all-to-all-start.3 = ((bf16[128,2,128]{2,1,0:T(2,128)(2,1)}), bf16[128,2,128]{2,1,0:T(2,128)(2,1)S(1)}, u32[]{:S(2)}, u32[]{:S(2)}) async-start(bf16[128,2,128]{2,1,0:T(2,128)(2,1)} %bitcast.11), calls=%async_computation.3 | async-start | bytes 131072 | tf_op jit(solution)/shard_map/all_to_all | solution.py:75
  40.0 3.7 %convolution_convert_fusion.1 = bf16[256,64,128]{2,0,1:T(8,128)(2,1)S(1)} fusion(bf16[128,64,128]{2,1,0:T(8,128)(2,1)} %convert_bitcast_fusion, s32[128]{0:T(128)S(1)} %multiply_add_fusion), kind=kOutput, calls=%fused_computation.8 | convolution fusion | flops 539000832 | bytes 6291968 | tf_op jit(solution)/shard_map/sb,bfo->sfo/dot_general | solution.py:65
  43.7 6.8 %copy.15 = bf16[128,2,64,128]{3,1,2,0:T(2,128)(2,1)} copy(bf16[128,2,64,128]{3,1,0,2:T(2,128)(2,1)S(1)} %bitcast.46) | data formatting | bytes 8388608 | tf_op jit(solution)/shard_map/reshape | solution.py:68
  50.5 12.7 %all-to-all-start = ((bf16[128,2,64,128]{3,1,2,0:T(2,128)(2,1)}), bf16[128,2,64,128]{3,1,2,0:T(2,128)(2,1)}, u32[]{:S(2)}, u32[]{:S(2)}) async-start(bf16[128,2,64,128]{3,1,2,0:T(2,128)(2,1)} %copy.15), calls=%async_computation | async-start | bytes 8388608 | tf_op jit(solution)/shard_map/all_to_all | solution.py:74
  63.7 0.8 reduce.4
  64.7 0.9 convolution_convert_fusion.2
  65.5 91.3 %all-to-all-done = bf16[128,2,64,128]{3,1,2,0:T(2,128)(2,1)} async-done(((bf16[128,2,64,128]{3,1,2,0:T(2,128)(2,1)}), bf16[128,2,64,128]{3,1,2,0:T(2,128)(2,1)}, u32[]{:S(2)}, u32[]{:S(2)}) %all-to-all-start) | async-done | bytes 4194336 | tf_op jit(solution)/shard_map/all_to_all | solution.py:74
  156.8 3.7 %all-to-all-start.4 = ((bf16[2,200,128]{2,1,0:T(8,128)(2,1)}), bf16[2,200,128]{2,1,0:T(8,128)(2,1)S(1)}, u32[]{:S(2)}, u32[]{:S(2)}) async-start(bf16[2,200,128]{2,1,0:T(8,128)(2,1)} %bitcast.13), calls=%async_computation.4 | async-start | bytes 204800 | tf_op jit(solution)/shard_map/all_to_all | solution.py:16
  160.6 6.8 %copy.16 = bf16[128,2,64,128]{3,1,0,2:T(2,128)(2,1)S(1)} copy(bf16[128,2,64,128]{3,1,2,0:T(2,128)(2,1)} %all-to-all-done) | data formatting | bytes 8388608 | tf_op jit(solution)/shard_map/all_to_all | solution.py:74
  167.3 1.9 convolution_convert_fusion
  169.2 3.2 %copy.31 = bf16[64,2,200,128]{3,2,0,1:T(8,128)(2,1)} copy(bf16[64,2,200,128]{3,2,1,0:T(8,128)(2,1)S(1)} %bitcast.45) | data formatting | bytes 13107200 | tf_op jit(solution)/shard_map/reshape | solution.py:11
  172.5 6.5 %all-to-all-start.2 = ((bf16[2,64,200,128]{3,2,1,0:T(8,128)(2,1)}), bf16[2,64,200,128]{3,2,1,0:T(8,128)(2,1)}, u32[]{:S(2)}, u32[]{:S(2)}) async-start(bf16[2,64,200,128]{3,2,1,0:T(8,128)(2,1)} %bitcast.43), calls=%async_computation.2 | async-start | bytes 13107200 | tf_op jit(solution)/shard_map/all_to_all | solution.py:16
  179.0 72.5 %all-to-all-done.2 = bf16[2,64,200,128]{3,2,1,0:T(8,128)(2,1)} async-done(((bf16[2,64,200,128]{3,2,1,0:T(8,128)(2,1)}), bf16[2,64,200,128]{3,2,1,0:T(8,128)(2,1)}, u32[]{:S(2)}, u32[]{:S(2)}) %all-to-all-start.2) | async-done | bytes 6553632 | tf_op jit(solution)/shard_map/all_to_all | solution.py:16
  251.5 4.7 %convert_reduce_fusion = f32[64,200,128]{2,1,0:T(8,128)S(1)} fusion(bf16[2,64,200,128]{3,2,1,0:T(8,128)(2,1)} %all-to-all-done.2), kind=kLoop, calls=%fused_computation | loop fusion | flops 4915200 | bytes 13107200 | tf_op jit(solution)/shard_map/reduce_sum | solution.py:17
  256.2 3.9 %fusion = f32[64,25600]{1,0:T(8,128)} fusion(f32[8,8,200,128]{3,2,1,0:T(8,128)S(1)} %bitcast.44, f32[25600]{0:T(1024)S(1)} %maximum_bitcast_fusion, f32[25600]{0:T(1024)S(1)} %convert_element_type.61), kind=kLoop, calls=%fused_computation.3 | loop fusion | flops 3276800 | bytes 13312000 | tf_op jit(solution)/shard_map/div | solution.py:88
  (14 shorter events, 0.7 us)
Async XLA Ops:
  0.0 22.9 %copy-start = (bf16[64,16384]{1,0:T(8,128)(2,1)S(1)}, bf16[64,16384]{1,0:T(8,128)(2,1)}, u32[]{:S(2)}) copy-start(bf16[64,16384]{1,0:T(8,128)(2,1)} %param.6) | copy-start | bytes 6291460
  3.2 24.6 %all-to-all-start.1 = ((s32[128,1,2]{2,1,0:T(1,128)}), s32[128,1,2]{2,1,0:T(1,128)S(1)}, u32[]{:S(2)}, u32[]{:S(2)}) async-start(s32[128,1,2]{2,1,0:T(1,128)} %bitcast.6), calls=%async_computation.1 | async-start | bytes 131072 | tf_op jit(solution)/shard_map/all_to_all | solution.py:76
  17.2 5.7 %copy-start.1 = (bf16[128,128,128]{2,1,0:T(8,128)(2,1)S(1)}, bf16[128,128,128]{2,1,0:T(8,128)(2,1)}, u32[]{:S(2)}) copy-start(bf16[128,128,128]{2,1,0:T(8,128)(2,1)} %param.7) | copy-start | bytes 12582916
  27.8 22.7 %all-to-all-start.3 = ((bf16[128,2,128]{2,1,0:T(2,128)(2,1)}), bf16[128,2,128]{2,1,0:T(2,128)(2,1)S(1)}, u32[]{:S(2)}, u32[]{:S(2)}) async-start(bf16[128,2,128]{2,1,0:T(2,128)(2,1)} %bitcast.11), calls=%async_computation.3 | async-start | bytes 131072 | tf_op jit(solution)/shard_map/all_to_all | solution.py:75
  50.5 106.3 %all-to-all-start = ((bf16[128,2,64,128]{3,1,2,0:T(2,128)(2,1)}), bf16[128,2,64,128]{3,1,2,0:T(2,128)(2,1)}, u32[]{:S(2)}, u32[]{:S(2)}) async-start(bf16[128,2,64,128]{3,1,2,0:T(2,128)(2,1)} %copy.15), calls=%async_computation | async-start | bytes 8388608 | tf_op jit(solution)/shard_map/all_to_all | solution.py:74
  156.8 15.6 %all-to-all-start.4 = ((bf16[2,200,128]{2,1,0:T(8,128)(2,1)}), bf16[2,200,128]{2,1,0:T(8,128)(2,1)S(1)}, u32[]{:S(2)}, u32[]{:S(2)}) async-start(bf16[2,200,128]{2,1,0:T(8,128)(2,1)} %bitcast.13), calls=%async_computation.4 | async-start | bytes 204800 | tf_op jit(solution)/shard_map/all_to_all | solution.py:16
  172.5 6.5 %copy-start.2 = (s32[25600]{0:T(1024)S(1)}, s32[25600]{0:T(1024)}, u32[]{:S(2)}) copy-start(s32[25600]{0:T(1024)} %param.11) | copy-start | bytes 307204
  172.5 79.0 %all-to-all-start.2 = ((bf16[2,64,200,128]{3,2,1,0:T(8,128)(2,1)}), bf16[2,64,200,128]{3,2,1,0:T(8,128)(2,1)}, u32[]{:S(2)}, u32[]{:S(2)}) async-start(bf16[2,64,200,128]{3,2,1,0:T(8,128)(2,1)} %bitcast.43), calls=%async_computation.2 | async-start | bytes 13107200 | tf_op jit(solution)/shard_map/all_to_all | solution.py:16
where the time goes:
time: 265 us; the launch traced here: 260 us
  waiting for transfers between devices  164 us (62%)
  starting transfers between devices  49.2 us (19%)
  local copies, waits for them, and re-layouts  18.2 us (7%)
  other arithmetic  17.5 us (7%)
  matrix products  11.3 us (4%)
    all_to_all x1, waiting for transfers between devices, per_device(): lax.all_to_all(sent_partial, 'band', split_axis=0, concat_axis=0, tiled=T...  91.3 us
    all_to_all x2, waiting for transfers between devices, sent_and_summed(): pieces = lax.all_to_all(cut_along(shard, dim, size), axis, 0, 0, tiled=True)  72.5 us
    all_to_all x1, starting transfers between devices, per_device(): lax.all_to_all(tile_sent, 'band', split_axis=0, concat_axis=0, tiled=True)  14 us
    all_to_all x1, starting transfers between devices, per_device(): lax.all_to_all(sent_partial, 'band', split_axis=0, concat_axis=0, tiled=T...  12.7 us
    all_to_all x1, starting transfers between devices, per_device(): lax.all_to_all(sent_covered, 'band', split_axis=0, concat_axis=0, tiled=T...  12.3 us
    all_to_all x2, starting transfers between devices, sent_and_summed(): pieces = lax.all_to_all(cut_along(shard, dim, size), axis, 0, 0, tiled=True)  10.2 us
    all_to_all x1, local copies, waits for them, and re-layouts, per_device(): lax.all_to_all(sent_partial, 'band', split_axis=0, concat_axis=0, tiled=T...  6.78 us
    reshape x1, local copies, waits for them, and re-layouts, per_device(): sent_partial.reshape(band_count, capacity, fields, tile_cells)  6.76 us
  transfers between devices with their start and end apart: 5, of which 2 were waited for; matrix products, arithmetic and copies ran while one was open for 14% of the time, Pallas kernels for 0%

commit v1 on v0

v1 whole, which is shorter than its diff:
```python
import functools

import jax
import jax.numpy as jnp
from jax import lax
from jax.experimental import pallas as pl
from jax.experimental.pallas import tpu as pltpu
from jax.sharding import PartitionSpec as P

cover_floor = 0.5
MESH = pl.DeviceIdType.MESH
CAP = 2
XLO = 2
X = 4
R = 8
ROWS = 8
CODE = 32


def place():
    band, sub = lax.axis_index("band"), lax.axis_index("sub")
    z, x_lo, rem = band // (XLO * R), (band // R) % XLO, band % R
    return z, x_lo, rem, sub * XLO + x_lo


def pack_kernel(chunk, pieces, band_ref, tile_ref, values_ref, weights_ref, mask_ref, out_ref, meta_ref, count_ref):
    step = pl.program_id(0)
    z, x_lo, rem, _ = place()
    lane_base = (z * R + rem) * CAP
    lanes = lax.broadcasted_iota(jnp.int32, (1, 128), 1)

    @pl.when(step == 0)
    def _():
        meta_ref[...] = jnp.zeros_like(meta_ref)

        def clear(i, _):
            count_ref[i] = 0
            return 0

        lax.fori_loop(0, count_ref.shape[0], clear, 0)

    fields = values_ref.shape[0]
    for i in range(chunk):
        block = step * chunk + i
        band, tile = band_ref[block], tile_ref[block] + 1
        rank = count_ref[band]
        count_ref[band] = rank + 1
        peer = (band // (XLO * R)) * R + band % R
        other = jnp.where((band // R) % XLO == x_lo, 0, 1)
        keep = mask_ref[i : i + 1, :].astype(jnp.float32).astype(jnp.bfloat16)
        left = values_ref[:, i * 128 : (i + 1) * 128] * keep
        left = jnp.concatenate([left, jnp.broadcast_to(keep, (16, 128))], axis=0)
        product = jnp.dot(left, weights_ref[i], preferred_element_type=jnp.float32)
        first = other * (CAP * pieces + 1) + rank * pieces
        out_ref[peer, pl.ds(first, pieces)] = product[:fields].reshape(pieces, ROWS, 128).astype(jnp.bfloat16)
        meta_ref[peer, pl.ds(other * CAP + rank, 1), :] = product[fields : fields + 1]
        here = lanes == lane_base + rank
        high = jnp.where(here, (tile // CODE).astype(jnp.float32), 0.0)
        low = jnp.where(here, (tile % CODE).astype(jnp.float32), 0.0)
        row = 4 + other * 2
        meta_ref[peer, pl.ds(row, 1), :] += high
        meta_ref[peer, pl.ds(row + 1, 1), :] += low

    @pl.when(step == pl.num_programs(0) - 1)
    def _():
        out_ref[:, CAP * pieces] = meta_ref[...].astype(jnp.bfloat16)


def exchange_kernel(peers, pieces, send_ref, near_ref, far_ref, self_sem, send_sem, recv_sem, far_send, far_recv):
    half = CAP * pieces + 1
    planes = peers // R
    z, x_lo, rem, x = place()
    me = z * R + rem

    def yz_device(z_to, rem_to):
        return {"band": z_to * (XLO * R) + x_lo * R + rem_to, "sub": x // XLO}

    def x_device(shift):
        x_to = (x + shift) % X
        return {"band": z * (XLO * R) + (x_to % XLO) * R + rem, "sub": x_to // XLO}

    def offset(step):
        q = step // R
        dz = ((q % 2) * ((q + 1) // 2) + (1 - q % 2) * (planes - q // 2)) % planes
        return dz, step % R

    barrier = pltpu.get_barrier_semaphore()

    def greet(step, _):
        dz, dr = offset(step)
        pl.semaphore_signal(barrier, inc=1, device_id=yz_device((z + dz) % planes, (rem + dr) % R), device_id_type=MESH)
        return 0

    lax.fori_loop(1, peers, greet, 0)
    for shift in range(1, X):
        pl.semaphore_signal(barrier, inc=1, device_id=x_device(shift), device_id_type=MESH)
    own = pltpu.make_async_copy(send_ref.at[me], near_ref.at[me], self_sem)
    own.start()
    pl.semaphore_wait(barrier, peers - 1 + X - 1)

    def send(step, _):
        dz, dr = offset(step)
        z_to, rem_to = (z + dz) % planes, (rem + dr) % R
        pltpu.make_async_remote_copy(
            src_ref=send_ref.at[z_to * R + rem_to],
            dst_ref=near_ref.at[me],
            send_sem=send_sem,
            recv_sem=recv_sem.at[me],
            device_id=yz_device(z_to, rem_to),
            device_id_type=MESH,
        ).start()
        return 0

    lax.fori_loop(1, peers, send, 0)

    def forward(source):
        for way, shift in enumerate((1, X - 1, 2)):
            begin = half - 1 if way < 2 else 0
            pltpu.make_async_remote_copy(
                src_ref=near_ref.at[source, pl.ds(begin, half)],
                dst_ref=far_ref.at[way, source],
                send_sem=far_send.at[way],
                recv_sem=far_recv.at[way],
                device_id=x_device(shift),
                device_id_type=MESH,
            ).start()

    own.wait()
    forward(me)

    def relay(step, _):
        dz, dr = offset(step)
        source = ((z + planes - dz) % planes) * R + (rem + R - dr) % R
        pltpu.make_async_remote_copy(
            src_ref=send_ref.at[me],
            dst_ref=near_ref.at[source],
            send_sem=send_sem,
            recv_sem=recv_sem.at[source],
            device_id=x_device(1),
            device_id_type=MESH,
        ).wait_recv()
        forward(source)
        return 0

    lax.fori_loop(1, peers, relay, 0)
    pltpu.make_async_remote_copy(
        src_ref=send_ref.at[pl.ds(0, peers - 1)],
        dst_ref=near_ref.at[pl.ds(0, peers - 1)],
        send_sem=send_sem,
        recv_sem=recv_sem.at[0],
        device_id=x_device(1),
        device_id_type=MESH,
    ).wait_send()
    for way in range(3):
        pltpu.make_async_remote_copy(
            src_ref=far_ref.at[way],
            dst_ref=far_ref.at[way],
            send_sem=far_send.at[way],
            recv_sem=far_recv.at[way],
            device_id=x_device(1),
            device_id_type=MESH,
        ).wait()


def place_kernel(peers, pieces, near_ref, far_ref, ocean_ref, out_ref, slots, total, cover, codes, code_smem, in_sem, code_sem, out_sem):
    half = CAP * pieces + 1
    tiles = ocean_ref.shape[0]
    sub = lax.axis_index("sub")
    parts = 1 + far_ref.shape[0]
    loads = [pltpu.make_async_copy(near_ref.at[:, pl.ds(0, half)], slots.at[0], in_sem.at[0])]
    loads += [pltpu.make_async_copy(far_ref.at[w], slots.at[w + 1], in_sem.at[w + 1]) for w in range(parts - 1)]
    for load in loads:
        load.start()

    def clear(i, _):
        total[:, pl.ds(pl.multiple_of(i * 1280, 128), 1280)] = jnp.zeros((total.shape[0], 1280), jnp.float32)
        return 0

    lax.fori_loop(0, total.shape[1] // 1280, clear, 0)
    cover[...] = jnp.zeros_like(cover)
    codes[...] = jnp.zeros_like(codes)
    shape_of = [(0, half - 1, 0, 4), (1, 0, 2, 6), (1, 0, 2, 6), (0, half - 1, 0, 4)]
    for part, (_, meta, _, digit) in enumerate(shape_of):
        loads[part].wait()
        digits = jnp.sum(slots[part, :, meta].astype(jnp.float32), axis=0)
        number = digits[digit : digit + 1] * CODE + digits[digit + 1 : digit + 2]
        codes[part : part + 1, :] = number.astype(jnp.int32) - 1
    copy = pltpu.make_async_copy(codes, code_smem, code_sem)
    copy.start()
    copy.wait()
    for part, (first, meta, row, _) in enumerate(shape_of):

        def add(source, _, part=part, first=first, meta=meta, row=row):
            for k in range(CAP):
                tile = code_smem[part, source * CAP + k] - sub * tiles

                @pl.when((tile >= 0) & (tile < tiles))
                def _():
                    slot = slots[part, source, first + k * pieces : first + (k + 1) * pieces].astype(jnp.float32)
                    cells = pl.ds(pl.multiple_of(tile * 128, 128), 128)
                    total[:, cells] += slot.reshape(pieces * ROWS, 128)
                    sides = slots[part, source, meta].astype(jnp.float32)
                    cover[pl.ds(tile, 1), :] += sides[row + k : row + k + 1]

            return 0

        lax.fori_loop(0, peers, add, 0)

    group = 8
    steps = tiles // group

    def finish(i, _):
        for k in range(group):
            tile = i * group + k
            keep = ocean_ref[pl.ds(tile, 1), :].astype(jnp.float32)
            scale = keep / jnp.maximum(cover[pl.ds(tile, 1), :], cover_floor)
            cells = pl.ds(pl.multiple_of(tile * 128, 128), 128)
            total[:, cells] = total[:, cells] * scale
        cells = pl.ds(pl.multiple_of(i * group * 128, 128), group * 128)
        pltpu.make_async_copy(total.at[:, cells], out_ref.at[:, cells], out_sem).start()
        return 0

    lax.fori_loop(0, steps, finish, 0)
    pltpu.make_async_copy(total, out_ref, out_sem).wait()


def per_device(land_values, area_weights, land_mask, dest_band, dest_tile, ocean_mask):
    fields = land_values.shape[0]
    blocks, cells, tile_cells = area_weights.shape
    bands = lax.axis_size("band")
    peers = bands // XLO
    pieces = fields // ROWS
    half = CAP * pieces + 1
    tiles = ocean_mask.shape[0] // tile_cells
    chunk = 16
    send = pl.pallas_call(
        functools.partial(pack_kernel, chunk, pieces),
        grid_spec=pltpu.PrefetchScalarGridSpec(
            num_scalar_prefetch=2,
            grid=(blocks // chunk,),
            in_specs=[
                pl.BlockSpec((fields, chunk * cells), lambda s, *_: (0, s)),
                pl.BlockSpec((chunk, cells, tile_cells), lambda s, *_: (s, 0, 0)),
                pl.BlockSpec((chunk, cells), lambda s, *_: (s, 0)),
            ],
            out_specs=pl.BlockSpec((peers, 2 * half - 1, ROWS, tile_cells), lambda s, *_: (0, 0, 0, 0)),
            scratch_shapes=[
                pltpu.VMEM((peers, ROWS, tile_cells), jnp.float32),
                pltpu.SMEM((bands,), jnp.int32),
            ],
        ),
        out_shape=jax.ShapeDtypeStruct((peers, 2 * half - 1, ROWS, tile_cells), jnp.bfloat16),
        name="pack",
    )(dest_band.reshape(blocks), dest_tile, land_values, area_weights, land_mask.reshape(blocks, cells))
    near, far = pl.pallas_call(
        functools.partial(exchange_kernel, peers, pieces),
        in_specs=[pl.BlockSpec(memory_space=pl.ANY)],
        out_specs=[pl.BlockSpec(memory_space=pl.ANY)] * 2,
        out_shape=[
            jax.ShapeDtypeStruct(send.shape, jnp.bfloat16),
            jax.ShapeDtypeStruct((X - 1, peers, half, ROWS, tile_cells), jnp.bfloat16),
        ],
        scratch_shapes=[
            pltpu.SemaphoreType.DMA,
            pltpu.SemaphoreType.DMA,
            pltpu.SemaphoreType.DMA((peers,)),
            pltpu.SemaphoreType.DMA((X - 1,)),
            pltpu.SemaphoreType.DMA((X - 1,)),
        ],
        compiler_params=pltpu.CompilerParams(collective_id=0, has_side_effects=True),
        name="exchange",
    )(send)
    return pl.pallas_call(
        functools.partial(place_kernel, peers, pieces),
        in_specs=[
            pl.BlockSpec(memory_space=pl.ANY),
            pl.BlockSpec(memory_space=pl.ANY),
            pl.BlockSpec(memory_space=pltpu.VMEM),
        ],
        out_specs=pl.BlockSpec(memory_space=pl.ANY),
        out_shape=jax.ShapeDtypeStruct((fields, tiles * tile_cells), jnp.float32),
        scratch_shapes=[
            pltpu.VMEM((X, peers, half, ROWS, tile_cells), jnp.bfloat16),
            pltpu.VMEM((fields, tiles * tile_cells), jnp.float32),
            pltpu.VMEM((tiles, tile_cells), jnp.float32),
            pltpu.VMEM((8, 128), jnp.int32),
            pltpu.SMEM((8, 128), jnp.int32),
            pltpu.SemaphoreType.DMA((X,)),
            pltpu.SemaphoreType.DMA,
            pltpu.SemaphoreType.DMA,
        ],
        compiler_params=pltpu.CompilerParams(vmem_limit_bytes=40 << 20),
        name="place",
    )(near, far, ocean_mask.reshape(tiles, tile_cells))


def solution(mesh):
    in_specs = (
        P(None, ("band", "sub")),
        P(("band", "sub"), None, None),
        P(("band", "sub")),
        P(("band", "sub"), None),
        P(("band", "sub")),
        P(("band", "sub")),
    )
    return jax.shard_map(
        per_device, mesh=mesh, in_specs=in_specs, out_specs=P(None, ("band", "sub")), check_vma=False
    )
```

time: 265 us -> 169 us (0.64)
  the two profiles are of different devices: /device:TPU:17 before, /device:TPU:136 now
where the time goes in v1:
time: 169 us
  Pallas kernels  164 us (97%)
  local copies, waits for them, and re-layouts  5.12 us (3%)
    pallas_call x1, Pallas kernels, per_device(): pl.pallas_call(functools.partial(exchange_kernel, peers, pieces), in_spec...  139 us
    pallas_call x1, Pallas kernels, per_device(): pl.pallas_call(functools.partial(place_kernel, peers, pieces), in_specs=[...  13.9 us
    pallas_call x1, Pallas kernels, per_device(): pl.pallas_call(functools.partial(pack_kernel, chunk, pieces), grid_spec=p...  11 us
    unnamed x6, local copies, waits for them, and re-layouts  5.12 us

profile of v1, /device:TPU:136, one launch (start us, length us, event | category | flops | bytes accessed | tf_op | source)
XLA Modules:
  0.0 168.7 jit_solution(13706002501030056449)
XLA Ops:
  0.0 11.0 %pack.1.send_ref = bf16[64,33,8,128]{3,2,1,0:T(8,128)(2,1)} custom-call(s32[128]{0:T(128)} %bitcast.5, s32[128]{0:T(128)} %tile_ref.1, bf16[64,16384]{1,0:T(8,128)(2,1)} %values_ref.1, bf16[128,128,128]{2,1,0:T(8,128)(2,1)} %weights_ref.1, s32[128,128]{1,0:T(8,128)} %bitcast.4), custom_call_target="tpu_custom_call" | custom-call | tf_op jit(solution)/shard_map/pack/pallas_call | solution.py:236
  11.0 0.0 copy-start.2
  11.0 138.6 %exchange.1 = (bf16[64,33,8,128]{3,2,1,0:T(8,128)(2,1)}, bf16[3,64,17,8,128]{4,3,2,1,0:T(8,128)(2,1)}) custom-call(bf16[64,33,8,128]{3,2,1,0:T(8,128)(2,1)} %pack.1.send_ref), custom_call_target="tpu_custom_call" | custom-call | tf_op jit(solution)/shard_map/exchange/pallas_call | solution.py:255
  149.7 0.0 copy-done.2
  149.7 0.0 copy-start
  149.7 2.9 %copy-done = bf16[3,64,17,8,128]{4,3,2,1,0:T(8,128)(2,1)S(1)} copy-done((bf16[3,64,17,8,128]{4,3,2,1,0:T(8,128)(2,1)S(1)}, bf16[3,64,17,8,128]{4,3,2,1,0:T(8,128)(2,1)}, u32[]{:S(2)}) %copy-start) | copy-done | bytes 6684696
  152.6 0.0 copy-start.1
  152.6 2.2 %copy-done.1 = bf16[64,33,8,128]{3,2,1,0:T(8,128)(2,1)S(1)} copy-done((bf16[64,33,8,128]{3,2,1,0:T(8,128)(2,1)S(1)}, bf16[64,33,8,128]{3,2,1,0:T(8,128)(2,1)}, u32[]{:S(2)}) %copy-start.1) | copy-done | bytes 4325400
  154.8 13.9 %place.1 = f32[64,25600]{1,0:T(8,128)} custom-call(bf16[64,33,8,128]{3,2,1,0:T(8,128)(2,1)S(1)} %copy-done.1, bf16[3,64,17,8,128]{4,3,2,1,0:T(8,128)(2,1)S(1)} %copy-done, s32[200,128]{1,0:T(8,128)S(1)} %bitcast.3), custom_call_target="tpu_custom_call" | custom-call | tf_op jit(solution)/shard_map/place/pallas_call | solution.py:273
Async XLA Ops:
  11.0 138.7 %copy-start.2 = (s32[25600]{0:T(1024)S(1)}, s32[25600]{0:T(1024)}, u32[]{:S(2)}) copy-start(s32[25600]{0:T(1024)} %param.11) | copy-start | bytes 307204
  149.7 2.9 %copy-start = (bf16[3,64,17,8,128]{4,3,2,1,0:T(8,128)(2,1)S(1)}, bf16[3,64,17,8,128]{4,3,2,1,0:T(8,128)(2,1)}, u32[]{:S(2)}) copy-start(bf16[3,64,17,8,128]{4,3,2,1,0:T(8,128)(2,1)} %get-tuple-element.8.far_ref) | copy-start | bytes 20054020
  152.6 2.2 %copy-start.1 = (bf16[64,33,8,128]{3,2,1,0:T(8,128)(2,1)S(1)}, bf16[64,33,8,128]{3,2,1,0:T(8,128)(2,1)}, u32[]{:S(2)}) copy-start(bf16[64,33,8,128]{3,2,1,0:T(8,128)(2,1)} %get-tuple-element.7.near_ref) | copy-start | bytes 12976132

commit v2 on v1

v2 whole, which is shorter than its diff:
```python
import functools

import jax
import jax.numpy as jnp
from jax import lax
from jax.experimental import pallas as pl
from jax.experimental.pallas import tpu as pltpu
from jax.sharding import PartitionSpec as P

cover_floor = 0.5
MESH = pl.DeviceIdType.MESH
CAP = 2
XLO = 2
X = 4
R = 8
ROWS = 8
CODE = 32


def place():
    band, sub = lax.axis_index("band"), lax.axis_index("sub")
    z, x_lo, rem = band // (XLO * R), (band // R) % XLO, band % R
    return z, x_lo, rem, sub * XLO + x_lo


def pack_kernel(chunk, pieces, planes, band_ref, tile_ref, values_ref, weights_ref, mask_ref, out_ref, meta_ref, count_ref):
    step = pl.program_id(0)
    z, x_lo, rem, _ = place()
    lanes = lax.broadcasted_iota(jnp.int32, (1, 128), 1)

    @pl.when(step == 0)
    def _():
        meta_ref[...] = jnp.zeros_like(meta_ref)

        def clear(i, _):
            count_ref[i] = 0
            return 0

        lax.fori_loop(0, count_ref.shape[0], clear, 0)

    fields = values_ref.shape[0]
    for i in range(chunk):
        block = step * chunk + i
        band, tile = band_ref[block], tile_ref[block] + 1
        rank = count_ref[band]
        count_ref[band] = rank + 1
        ahead = (band // (XLO * R) + planes - z) % planes
        peer = ahead * R + band % R
        other = jnp.where((band // R) % XLO == x_lo, 0, 1)
        keep = mask_ref[i : i + 1, :].astype(jnp.float32).astype(jnp.bfloat16)
        left = values_ref[:, i * 128 : (i + 1) * 128] * keep
        left = jnp.concatenate([left, jnp.broadcast_to(keep, (16, 128))], axis=0)
        product = jnp.dot(left, weights_ref[i], preferred_element_type=jnp.float32)
        first = other * (CAP * pieces + 1) + rank * pieces
        out_ref[peer, pl.ds(first, pieces)] = product[:fields].reshape(pieces, ROWS, 128).astype(jnp.bfloat16)
        meta_ref[peer, pl.ds(other * CAP + rank, 1), :] = product[fields : fields + 1]
        here = lanes == (ahead * R + rem) * CAP + rank
        high = jnp.where(here, (tile // CODE).astype(jnp.float32), 0.0)
        low = jnp.where(here, (tile % CODE).astype(jnp.float32), 0.0)
        row = 4 + other * 2
        meta_ref[peer, pl.ds(row, 1), :] += high
        meta_ref[peer, pl.ds(row + 1, 1), :] += low

    @pl.when(step == pl.num_programs(0) - 1)
    def _():
        out_ref[:, CAP * pieces] = meta_ref[...].astype(jnp.bfloat16)


SOURCES = ((0, 0), (0, 1), (1, 0), (-1, 0), (1, 1), (-1, 1), (2, 0), (2, 1))
HOPS = [(far, hop) for far in range(1, 5) for hop in range(1, far + 1)]


def exchange_kernel(pieces, send_ref, near_ref, far_ref, held, relay, self_sem, y_send, y_recv, z_send, z_recv, x_send, x_recv):
    half = CAP * pieces + 1
    planes = near_ref.shape[0]
    z, x_lo, rem, x = place()
    y, core = rem // 2, rem % 2
    ring_y = R // 2

    def device(z_to=z, rem_to=rem, x_to=x):
        return {"band": z_to * (XLO * R) + (x_to % XLO) * R + rem_to, "sub": x_to // XLO}

    def mate(index, sign):
        dy, dc = SOURCES[index]
        return ((y + ring_y + sign * dy) % ring_y) * 2 + (core + dc) % 2

    right, left = (z + 1) % planes, (z + planes - 1) % planes
    ways = (1, X - 1, 2)

    barrier = pltpu.get_barrier_semaphore()
    greeted = [device(rem_to=mate(i, 1)) for i in range(1, R)] + [device(z_to=right), device(z_to=left)]
    greeted += [device(x_to=(x + shift) % X) for shift in ways]
    for peer in greeted:
        pl.semaphore_signal(barrier, inc=1, device_id=peer, device_id_type=MESH)
    own = [
        pltpu.make_async_copy(send_ref.at[0, rem], near_ref.at[0, rem], self_sem.at[0]),
        pltpu.make_async_copy(send_ref.at[pl.ds(1, planes - 1), rem], held.at[:, rem], self_sem.at[1]),
    ]
    for copy in own:
        copy.start()
    pl.semaphore_wait(barrier, len(greeted))

    def remote(src, dst, send_sem, recv_sem, peer):
        return pltpu.make_async_remote_copy(
            src_ref=src, dst_ref=dst, send_sem=send_sem, recv_sem=recv_sem, device_id=peer, device_id_type=MESH
        )

    def y_copy(i, onward):
        to = mate(i, 1)
        src = send_ref.at[pl.ds(1, planes - 1), to] if onward else send_ref.at[0, to]
        dst = held.at[:, rem] if onward else near_ref.at[0, rem]
        return remote(src, dst, y_send.at[onward], y_recv.at[onward, i], device(rem_to=to))

    for i in range(1, R):
        for onward in (1, 0):
            y_copy(i, onward).start()

    def forward(ahead, source):
        for way, shift in enumerate(ways):
            begin = half - 1 if way < 2 else 0
            remote(
                near_ref.at[ahead, source, pl.ds(begin, half)],
                far_ref.at[way, ahead, source],
                x_send.at[way],
                x_recv.at[way],
                device(x_to=(x + shift) % X),
            ).start()

    def travels(i, way, far):
        return far < 4 or i % 2 == way

    def z_copy(i, way, far, hop):
        source = mate(i, -1)
        at = far if way == 0 else planes - far
        slot = (far - 1) * (far - 2) // 2
        src = held.at[at - 1, source] if hop == 1 else relay.at[way, i, slot + hop - 2]
        dst = near_ref.at[at, source] if hop == far else relay.at[way, i, slot + hop - 1]
        sem = z_recv.at[way, i, HOPS.index((far, hop))]
        return remote(src, dst, z_send.at[way], sem, device(z_to=right if way == 0 else left))

    def arrive(i, way, far, hop):
        z_copy(i, way, far, hop).wait_recv()
        if hop == far:
            forward(far if way == 0 else planes - far, mate(i, -1))
        else:
            z_copy(i, way, far, hop + 1).start()

    for turn in range(R + 4):
        if turn < R:
            if turn == 0:
                own[1].wait()
            else:
                y_copy(turn, 1).wait_recv()
            for far in (1, 2, 3, 4):
                for way in (0, 1):
                    if travels(turn, way, far):
                        z_copy(turn, way, far, 1).start()
            if turn == 0:
                own[0].wait()
            else:
                y_copy(turn, 0).wait_recv()
            forward(0, mate(turn, -1))
        for hop in (4, 3, 2, 1):
            i = turn - hop
            if 0 <= i < R:
                for far in range(hop, 5):
                    for way in (0, 1):
                        if travels(i, way, far):
                            arrive(i, way, far, hop)

    remote(near_ref.at[0, pl.ds(0, R - 1)], near_ref.at[0, pl.ds(0, R - 1)], y_send.at[0], y_recv.at[0, 0], device()).wait_send()
    remote(held.at[:, pl.ds(0, R - 1)], held.at[:, pl.ds(0, R - 1)], y_send.at[1], y_recv.at[0, 0], device()).wait_send()
    for way in (0, 1):
        remote(near_ref, near_ref, z_send.at[way], y_recv.at[0, 0], device()).wait_send()
    for way in range(X - 1):
        remote(far_ref.at[way], far_ref.at[way], x_send.at[way], x_recv.at[way], device()).wait()


def place_kernel(pieces, near_ref, far_ref, ocean_ref, out_ref, total, cover, codes, code_smem, code_sem, out_sem):
    half = CAP * pieces + 1
    tiles = ocean_ref.shape[0]
    planes = near_ref.shape[0]
    sub = lax.axis_index("sub")
    parts = [((), 0, half - 1, 0, 4), ((0,), 1, 0, 2, 6), ((1,), 1, 0, 2, 6), ((2,), 0, half - 1, 0, 4)]
    refs = [near_ref] + [far_ref] * (X - 1)

    codes[...] = jnp.zeros_like(codes)
    for part, (at, _, meta, _, digit) in enumerate(parts):
        sides = refs[part][(*at, slice(None), slice(None), meta)].astype(jnp.float32)
        digits = jnp.sum(sides.reshape(planes * R, ROWS, 128), axis=0)
        number = digits[digit : digit + 1] * CODE + digits[digit + 1 : digit + 2]
        codes[part : part + 1, :] = number.astype(jnp.int32) - 1
    copy = pltpu.make_async_copy(codes, code_smem, code_sem)
    copy.start()

    def clear(i, _):
        total[:, pl.ds(pl.multiple_of(i * 1280, 128), 1280)] = jnp.zeros((total.shape[0], 1280), jnp.float32)
        return 0

    lax.fori_loop(0, total.shape[1] // 1280, clear, 0)
    cover[...] = jnp.zeros_like(cover)
    copy.wait()
    for part, (at, first, meta, row, _) in enumerate(parts):

        def add(source, _, part=part, at=at, first=first, meta=meta, row=row):
            where = (*at, source // R, source % R)
            for k in range(CAP):
                tile = code_smem[part, source * CAP + k] - sub * tiles

                @pl.when((tile >= 0) & (tile < tiles))
                def _():
                    begin = first + k * pieces
                    slot = refs[part][(*where, slice(begin, begin + pieces))].astype(jnp.float32)
                    cells = pl.ds(pl.multiple_of(tile * 128, 128), 128)
                    total[:, cells] += slot.reshape(pieces * ROWS, 128)
                    sides = refs[part][(*where, meta)].astype(jnp.float32)
                    cover[pl.ds(tile, 1), :] += sides[row + k : row + k + 1]

            return 0

        lax.fori_loop(0, planes * R, add, 0)

    group = 8
    steps = tiles // group

    def finish(i, _):
        for k in range(group):
            tile = i * group + k
            keep = ocean_ref[pl.ds(tile, 1), :].astype(jnp.float32)
            scale = keep / jnp.maximum(cover[pl.ds(tile, 1), :], cover_floor)
            cells = pl.ds(pl.multiple_of(tile * 128, 128), 128)
            total[:, cells] = total[:, cells] * scale
        cells = pl.ds(pl.multiple_of(i * group * 128, 128), group * 128)
        pltpu.make_async_copy(total.at[:, cells], out_ref.at[:, cells], out_sem).start()
        return 0

    lax.fori_loop(0, steps, finish, 0)
    pltpu.make_async_copy(total, out_ref, out_sem).wait()


def per_device(land_values, area_weights, land_mask, dest_band, dest_tile, ocean_mask):
    fields = land_values.shape[0]
    blocks, cells, tile_cells = area_weights.shape
    bands = lax.axis_size("band")
    planes = bands // (XLO * R)
    pieces = fields // ROWS
    half = CAP * pieces + 1
    tiles = ocean_mask.shape[0] // tile_cells
    chunk = 16
    unit = (2 * half - 1, ROWS, tile_cells)
    send = pl.pallas_call(
        functools.partial(pack_kernel, chunk, pieces, planes),
        grid_spec=pltpu.PrefetchScalarGridSpec(
            num_scalar_prefetch=2,
            grid=(blocks // chunk,),
            in_specs=[
                pl.BlockSpec((fields, chunk * cells), lambda s, *_: (0, s)),
                pl.BlockSpec((chunk, cells, tile_cells), lambda s, *_: (s, 0, 0)),
                pl.BlockSpec((chunk, cells), lambda s, *_: (s, 0)),
            ],
            out_specs=pl.BlockSpec((planes * R, *unit), lambda s, *_: (0, 0, 0, 0)),
            scratch_shapes=[
                pltpu.VMEM((planes * R, ROWS, tile_cells), jnp.float32),
                pltpu.SMEM((bands,), jnp.int32),
            ],
        ),
        out_shape=jax.ShapeDtypeStruct((planes * R, *unit), jnp.bfloat16),
        name="pack",
    )(dest_band.reshape(blocks), dest_tile, land_values, area_weights, land_mask.reshape(blocks, cells))
    near, far = pl.pallas_call(
        functools.partial(exchange_kernel, pieces),
        in_specs=[pl.BlockSpec(memory_space=pl.ANY)],
        out_specs=[pl.BlockSpec(memory_space=pl.ANY)] * 2,
        out_shape=[
            pltpu.VMEM((planes, R, *unit), jnp.bfloat16),
            pltpu.VMEM((X - 1, planes, R, half, ROWS, tile_cells), jnp.bfloat16),
        ],
        scratch_shapes=[
            pltpu.VMEM((planes - 1, R, *unit), jnp.bfloat16),
            pltpu.VMEM((2, R, 6, *unit), jnp.bfloat16),
            pltpu.SemaphoreType.DMA((2,)),
            pltpu.SemaphoreType.DMA((2,)),
            pltpu.SemaphoreType.DMA((2, R)),
            pltpu.SemaphoreType.DMA((2,)),
            pltpu.SemaphoreType.DMA((2, R, len(HOPS))),
            pltpu.SemaphoreType.DMA((X - 1,)),
            pltpu.SemaphoreType.DMA((X - 1,)),
        ],
        compiler_params=pltpu.CompilerParams(collective_id=0, has_side_effects=True, vmem_limit_bytes=16 << 20),
        name="exchange",
    )(send.reshape(planes, R, *unit))
    return pl.pallas_call(
        functools.partial(place_kernel, pieces),
        in_specs=[pl.BlockSpec(memory_space=pltpu.VMEM)] * 3,
        out_specs=pl.BlockSpec(memory_space=pl.ANY),
        out_shape=jax.ShapeDtypeStruct((fields, tiles * tile_cells), jnp.float32),
        scratch_shapes=[
            pltpu.VMEM((fields, tiles * tile_cells), jnp.float32),
            pltpu.VMEM((tiles, tile_cells), jnp.float32),
            pltpu.VMEM((8, 128), jnp.int32),
            pltpu.SMEM((8, 128), jnp.int32),
            pltpu.SemaphoreType.DMA,
            pltpu.SemaphoreType.DMA,
        ],
        compiler_params=pltpu.CompilerParams(vmem_limit_bytes=24 << 20),
        name="place",
    )(near, far, ocean_mask.reshape(tiles, tile_cells))


def solution(mesh):
    in_specs = (
        P(None, ("band", "sub")),
        P(("band", "sub"), None, None),
        P(("band", "sub")),
        P(("band", "sub"), None),
        P(("band", "sub")),
        P(("band", "sub")),
    )
    return jax.shard_map(
        per_device, mesh=mesh, in_specs=in_specs, out_specs=P(None, ("band", "sub")), check_vma=False
    )
```

time: 169 us -> 149 us (0.88)
  the two profiles are of different devices: /device:TPU:136 before, /device:TPU:17 now
where the time goes in v2:
time: 149 us; the launch traced here: 150 us
  Pallas kernels  147 us (99%)
  local copies, waits for them, and re-layouts  2.23 us (1%)
    pallas_call x1, Pallas kernels, per_device(): pl.pallas_call(functools.partial(exchange_kernel, pieces), in_specs=[pl.B...  123 us
    pallas_call x1, Pallas kernels, per_device(): pl.pallas_call(functools.partial(place_kernel, pieces), in_specs=[pl.Bloc...  13.4 us
    pallas_call x1, Pallas kernels, per_device(): pl.pallas_call(functools.partial(pack_kernel, chunk, pieces, planes), gri...  11.1 us

profile of v2, /device:TPU:17, one launch (start us, length us, event | category | flops | bytes accessed | tf_op | source)
XLA Modules:
  0.0 149.6 jit_solution(5591964327714563204)
XLA Ops:
  0.0 11.1 %pack.1 = bf16[64,33,8,128]{3,2,1,0:T(8,128)(2,1)} custom-call(s32[128]{0:T(128)} %bitcast.7, s32[128]{0:T(128)} %tile_ref.1, bf16[64,16384]{1,0:T(8,128)(2,1)} %values_ref.1, bf16[128,128,128]{2,1,0:T(8,128)(2,1)} %weights_ref.1, s32[128,128]{1,0:T(8,128)} %bitcast.6), custom_call_target="tpu_custom_call" | custom-call | tf_op jit(solution)/shard_map/pack/pallas_call | solution.py:251
  11.1 0.0 copy-start
  11.1 2.2 %copy-done = bf16[64,33,8,128]{3,2,1,0:T(8,128)(2,1)S(1)} copy-done((bf16[64,33,8,128]{3,2,1,0:T(8,128)(2,1)S(1)}, bf16[64,33,8,128]{3,2,1,0:T(8,128)(2,1)}, u32[]{:S(2)}) %copy-start) | copy-done | bytes 4325400
  13.3 0.0 copy-start.1
  13.3 122.9 %exchange.1 = (bf16[8,8,33,8,128]{4,3,2,1,0:T(8,128)(2,1)S(1)}, bf16[3,8,8,17,8,128]{5,4,3,2,1,0:T(8,128)(2,1)S(1)}) custom-call(bf16[8,8,33,8,128]{4,3,2,1,0:T(8,128)(2,1)S(1)} %bitcast.4), custom_call_target="tpu_custom_call" | custom-call | tf_op jit(solution)/shard_map/exchange/pallas_call | solution.py:270
  136.2 0.0 copy-done.1
  136.2 13.4 %place.1 = f32[64,25600]{1,0:T(8,128)} custom-call(bf16[8,8,33,8,128]{4,3,2,1,0:T(8,128)(2,1)S(1)} %get-tuple-element.7.near_ref, bf16[3,8,8,17,8,128]{5,4,3,2,1,0:T(8,128)(2,1)S(1)} %get-tuple-element.8.far_ref, s32[200,128]{1,0:T(8,128)S(1)} %bitcast.5), custom_call_target="tpu_custom_call" | custom-call | tf_op jit(solution)/shard_map/place/pallas_call | solution.py:292
Async XLA Ops:
  11.1 2.2 %copy-start = (bf16[64,33,8,128]{3,2,1,0:T(8,128)(2,1)S(1)}, bf16[64,33,8,128]{3,2,1,0:T(8,128)(2,1)}, u32[]{:S(2)}) copy-start(bf16[64,33,8,128]{3,2,1,0:T(8,128)(2,1)} %pack.1) | copy-start | bytes 12976132
  13.3 122.9 %copy-start.1 = (s32[25600]{0:T(1024)S(1)}, s32[25600]{0:T(1024)}, u32[]{:S(2)}) copy-start(s32[25600]{0:T(1024)} %param.11) | copy-start | bytes 307204

commit v3 on v2

v3 whole, which is shorter than its diff:
```python
import functools

import jax
import jax.numpy as jnp
from jax import lax
from jax.experimental import pallas as pl
from jax.experimental.pallas import tpu as pltpu
from jax.sharding import PartitionSpec as P

cover_floor = 0.5
MESH = pl.DeviceIdType.MESH
CAP = 2
XLO = 2
X = 4
R = 8
ROWS = 8
CODE = 32


def place():
    band, sub = lax.axis_index("band"), lax.axis_index("sub")
    z, x_lo, rem = band // (XLO * R), (band // R) % XLO, band % R
    return z, x_lo, rem, sub * XLO + x_lo


def table_kernel(band_ref, tile_ref, out_ref):
    blocks = band_ref.shape[1]
    down = lax.broadcasted_iota(jnp.int32, (blocks, blocks), 0)
    across = lax.broadcasted_iota(jnp.int32, (blocks, blocks), 1)
    band = jnp.broadcast_to(band_ref[...], (blocks, blocks))
    tile = jnp.broadcast_to(tile_ref[...], (blocks, blocks))
    band_down = jnp.sum(jnp.where(down == across, band, 0), axis=1, keepdims=True)
    tile_down = jnp.sum(jnp.where(down == across, tile, 0), axis=1, keepdims=True) + 1
    rank_down = jnp.sum(jnp.where((band == band_down) & (across < down), 1, 0), axis=1, keepdims=True)
    slot_down = band_down * CAP + rank_down
    for part in range(CAP):
        here = slot_down == across + part * blocks
        for row, value in enumerate((down, tile_down // CODE, tile_down % CODE)):
            out_ref[row : row + 1, part * blocks : (part + 1) * blocks] = jnp.sum(
                jnp.where(here, value, 0), axis=0, keepdims=True
            )


SOURCES = ((0, 0), (0, 1), (1, 0), (-1, 0), (1, 1), (-1, 1), (2, 0), (2, 1))
HOPS = [(far, hop) for far in range(1, 5) for hop in range(1, far + 1)]


def exchange_kernel(
    pieces, table_ref, values_hbm, weights_hbm, mask_hbm, near_ref, far_ref,
    values_ref, weights_ref, mask_ref, in_sem, stage, held, relay, y_send, y_recv, z_send, z_recv, x_send, x_recv,
):
    loads = [
        pltpu.make_async_copy(weights_hbm, weights_ref, in_sem.at[1]),
        pltpu.make_async_copy(mask_hbm, mask_ref, in_sem.at[2]),
    ]
    for load in loads:
        load.start()

    def load_block(block, _):
        cells = pl.ds(pl.multiple_of(block * 128, 128), 128)
        pltpu.make_async_copy(values_hbm.at[:, cells], values_ref.at[block], in_sem.at[0]).start()
        return 0

    lax.fori_loop(0, values_ref.shape[0], load_block, 0)
    loads.append(pltpu.make_async_copy(values_ref, values_ref, in_sem.at[0]))
    half = CAP * pieces + 1
    planes = near_ref.shape[0]
    fields = values_ref.shape[1]
    z, x_lo, rem, x = place()
    y, core = rem // 2, rem % 2
    ring_y = R // 2
    row = lax.broadcasted_iota(jnp.int32, (ROWS, 128), 0)
    lane = lax.broadcasted_iota(jnp.int32, (ROWS, 128), 1)

    def device(z_to=z, rem_to=rem, x_to=x):
        return {"band": z_to * (XLO * R) + (x_to % XLO) * R + rem_to, "sub": x_to // XLO}

    def mate(index, sign):
        dy, dc = SOURCES[index]
        return ((y + ring_y + sign * dy) % ring_y) * 2 + (core + dc) % 2

    def fill(unit, ahead, to):
        start = ahead * R + rem
        sides = jnp.zeros((ROWS, 128), jnp.float32)
        for part in range(2):
            lo = x_lo if part == 0 else XLO - 1 - x_lo
            slot = (((z + ahead) % planes) * (XLO * R) + lo * R + to) * CAP
            for rank in range(CAP):
                block = table_ref[0, slot + rank]
                keep = mask_ref[block].astype(jnp.float32).astype(jnp.bfloat16)
                left = values_ref[block] * keep
                left = jnp.concatenate([left, jnp.broadcast_to(keep, (16, 128))], axis=0)
                product = jnp.dot(left, weights_ref[block], preferred_element_type=jnp.float32)
                first = part * half + rank * pieces
                unit[first : first + pieces] = product[:fields].reshape(pieces, ROWS, 128).astype(jnp.bfloat16)
                sides = jnp.where(row == part * CAP + rank, product[fields : fields + ROWS], sides)
                for digit in range(2):
                    here = (row == 4 + part * 2 + digit) & (lane == start + rank * planes * R)
                    sides = jnp.where(here, table_ref[1 + digit, slot + rank].astype(jnp.float32), sides)
        unit[half - 1] = sides.astype(jnp.bfloat16)

    def prepare(i):
        to = mate(i, 1)

        def one(ahead, _):
            fill(stage.at[i, ahead], ahead, to)
            return 0

        if i == 0:
            fill(near_ref.at[0, rem], 0, to)
            lax.fori_loop(1, planes, one, 0)
        else:
            lax.fori_loop(0, planes, one, 0)

    right, left = (z + 1) % planes, (z + planes - 1) % planes
    ways = (1, X - 1, 2)

    barrier = pltpu.get_barrier_semaphore()
    greeted = [device(rem_to=mate(i, 1)) for i in range(1, R)] + [device(z_to=right), device(z_to=left)]
    greeted += [device(x_to=(x + shift) % X) for shift in ways]
    for peer in greeted:
        pl.semaphore_signal(barrier, inc=1, device_id=peer, device_id_type=MESH)
    for load in loads:
        load.wait()
    prepare(0)
    prepare(1)
    pl.semaphore_wait(barrier, len(greeted))

    def remote(src, dst, send_sem, recv_sem, peer):
        return pltpu.make_async_remote_copy(
            src_ref=src, dst_ref=dst, send_sem=send_sem, recv_sem=recv_sem, device_id=peer, device_id_type=MESH
        )

    def y_copy(i, onward):
        to = mate(i, 1)
        src = stage.at[i, pl.ds(1, planes - 1)] if onward else stage.at[i, 0]
        dst = held.at[:, rem] if onward else near_ref.at[0, rem]
        return remote(src, dst, y_send.at[onward], y_recv.at[onward, i], device(rem_to=to))

    def y_start(i):
        for onward in (1, 0):
            y_copy(i, onward).start()

    def forward(ahead, source):
        for way, shift in enumerate(ways):
            begin = half - 1 if way < 2 else 0
            remote(
                near_ref.at[ahead, source, pl.ds(begin, half)],
                far_ref.at[way, ahead, source],
                x_send.at[way],
                x_recv.at[way],
                device(x_to=(x + shift) % X),
            ).start()

    def travels(i, way, far):
        return far < 4 or i % 2 == way

    def z_copy(i, way, far, hop):
        source = mate(i, -1)
        at = far if way == 0 else planes - far
        slot = (far - 1) * (far - 2) // 2
        first = stage.at[0, at] if i == 0 else held.at[at - 1, source]
        src = first if hop == 1 else relay.at[way, i, slot + hop - 2]
        dst = near_ref.at[at, source] if hop == far else relay.at[way, i, slot + hop - 1]
        sem = z_recv.at[way, i, HOPS.index((far, hop))]
        return remote(src, dst, z_send.at[way], sem, device(z_to=right if way == 0 else left))

    def arrive(i, way, far, hop):
        z_copy(i, way, far, hop).wait_recv()
        if hop == far:
            forward(far if way == 0 else planes - far, mate(i, -1))
        else:
            z_copy(i, way, far, hop + 1).start()

    prepared = 1
    for turn in range(R + 4):
        if turn < R:
            if turn > 0:
                y_copy(turn, 1).wait_recv()
            for far in (1, 2, 3, 4):
                for way in (0, 1):
                    if travels(turn, way, far):
                        z_copy(turn, way, far, 1).start()
            if turn > 0:
                y_copy(turn, 0).wait_recv()
            forward(0, mate(turn, -1))
        for _ in range(2 if turn < 2 else 1):
            if prepared < R:
                if prepared + 1 < R:
                    prepare(prepared + 1)
                y_start(prepared)
                prepared += 1
        for hop in (1, 2, 3, 4):
            i = turn - hop
            if 0 <= i < R:
                for far in range(hop, 5):
                    for way in (0, 1):
                        if travels(i, way, far):
                            arrive(i, way, far, hop)

    remote(near_ref.at[0, pl.ds(0, R - 1)], near_ref.at[0, pl.ds(0, R - 1)], y_send.at[0], y_recv.at[0, 0], device()).wait_send()
    remote(held.at[:, pl.ds(0, R - 1)], held.at[:, pl.ds(0, R - 1)], y_send.at[1], y_recv.at[0, 0], device()).wait_send()
    for way in (0, 1):
        remote(near_ref, near_ref, z_send.at[way], y_recv.at[0, 0], device()).wait_send()
    for way in range(X - 1):
        remote(far_ref.at[way], far_ref.at[way], x_send.at[way], x_recv.at[way], device()).wait()


def place_kernel(
    pieces, planes, near_ref, far_ref, ocean_ref, out_ref,
    total, scale, codes, code_smem, picked, code_sem, out_sem,
):
    half = CAP * pieces + 1
    tiles = ocean_ref.shape[0]
    sources = planes * R
    sub = lax.axis_index("sub")

    tile_down = lax.broadcasted_iota(jnp.int32, (tiles, sources), 0) + sub * tiles
    cover = jnp.zeros((tiles, 128), jnp.float32)
    for part in range(X):
        other = part in (1, 2)
        if part == 0:
            sides = near_ref.reshape(sources, 2 * half - 1, ROWS, 128)[:, half - 1]
        else:
            sides = far_ref.reshape(X - 1, sources, half, ROWS, 128)[part - 1, :, 0 if other else half - 1]
        sides = sides.astype(jnp.float32)
        digits = jnp.sum(sides, axis=0)
        digit = 6 if other else 4
        number = (digits[digit : digit + 1] * CODE + digits[digit + 1 : digit + 2]).astype(jnp.int32) - 1
        codes[part : part + 1, :] = number
        for rank in range(CAP):
            row = rank + (CAP if other else 0)
            chosen = tile_down == number[:, rank * sources : (rank + 1) * sources]
            chosen = jnp.where(chosen, 1.0, 0.0).astype(jnp.bfloat16)
            cover += jnp.dot(chosen, sides[:, row].astype(jnp.bfloat16), preferred_element_type=jnp.float32)
    copy = pltpu.make_async_copy(codes, code_smem, code_sem)
    copy.start()
    scale[...] = ocean_ref[...].astype(jnp.float32) / jnp.maximum(cover, cover_floor)

    def clear(i, _):
        total[:, pl.ds(pl.multiple_of(i * 1280, 128), 1280)] = jnp.zeros((total.shape[0], 1280), jnp.float32)
        return 0

    lax.fori_loop(0, tiles // 10, clear, 0)
    copy.wait()

    def pick(part, stride, offset, count):
        for rank in range(CAP):

            def one(step, count, rank=rank):
                for k in range(8):
                    source = step * 8 + k
                    tile = code_smem[part, rank * sources + source] - sub * tiles
                    start = offset + source * stride + rank * pieces
                    picked[count] = start * 256 + tile
                    count = count + jnp.where((tile >= 0) & (tile < tiles), 1, 0)
                return count

            count = lax.fori_loop(0, sources // 8, one, count)
        return count

    def add(ref, count):
        group = 4
        for k in range(group):
            picked[count + k] = tiles

        def several(step, _):
            slots = []
            for k in range(group):
                entry = picked[step * group + k]
                slot = ref[pl.ds(entry // 256, pieces)].astype(jnp.float32).reshape(pieces * ROWS, 128)
                slots.append((pl.ds(pl.multiple_of((entry % 256) * 128, 128), 128), slot))
            for cells, slot in slots:
                total[:, cells] += slot
            return 0

        lax.fori_loop(0, (count + group - 1) // group, several, 0)

    add(near_ref, pick(0, 2 * half - 1, 0, 0))
    count = pick(1, half, 1, 0)
    count = pick(2, half, sources * half + 1, count)
    add(far_ref, pick(3, half, 2 * sources * half, count))

    group = 8

    def finish(i, _):
        for k in range(group):
            tile = i * group + k
            cells = pl.ds(pl.multiple_of(tile * 128, 128), 128)
            total[:, cells] = total[:, cells] * scale[pl.ds(tile, 1), :]
        cells = pl.ds(pl.multiple_of(i * group * 128, 128), group * 128)
        pltpu.make_async_copy(total.at[:, cells], out_ref.at[:, cells], out_sem).start()
        return 0

    lax.fori_loop(0, tiles // group, finish, 0)
    pltpu.make_async_copy(total.at[:, pl.ds(0, tiles * 128)], out_ref, out_sem).wait()


def per_device(land_values, area_weights, land_mask, dest_band, dest_tile, ocean_mask):
    fields = land_values.shape[0]
    blocks, cells, tile_cells = area_weights.shape
    bands = lax.axis_size("band")
    planes = bands // (XLO * R)
    pieces = fields // ROWS
    half = CAP * pieces + 1
    tiles = ocean_mask.shape[0] // tile_cells
    unit = (2 * half - 1, ROWS, tile_cells)
    table = pl.pallas_call(
        table_kernel,
        in_specs=[pl.BlockSpec(memory_space=pltpu.VMEM)] * 2,
        out_specs=pl.BlockSpec(memory_space=pltpu.VMEM),
        out_shape=jax.ShapeDtypeStruct((3, bands * CAP), jnp.int32),
        name="table",
    )(dest_band.reshape(1, blocks), dest_tile.reshape(1, blocks))
    near, far = pl.pallas_call(
        functools.partial(exchange_kernel, pieces),
        in_specs=[
            pl.BlockSpec(memory_space=pltpu.SMEM),
            pl.BlockSpec(memory_space=pltpu.HBM),
            pl.BlockSpec(memory_space=pltpu.HBM),
            pl.BlockSpec(memory_space=pltpu.HBM),
        ],
        out_specs=[pl.BlockSpec(memory_space=pltpu.VMEM)] * 2,
        out_shape=[
            pltpu.VMEM((planes, R, *unit), jnp.bfloat16),
            pltpu.VMEM((X - 1, planes, R, half, ROWS, tile_cells), jnp.bfloat16),
        ],
        scratch_shapes=[
            pltpu.VMEM((blocks, fields, cells), jnp.bfloat16),
            pltpu.VMEM(area_weights.shape, jnp.bfloat16),
            pltpu.VMEM((blocks, 1, cells), jnp.int32),
            pltpu.SemaphoreType.DMA((3,)),
            pltpu.VMEM((R, planes, *unit), jnp.bfloat16),
            pltpu.VMEM((planes - 1, R, *unit), jnp.bfloat16),
            pltpu.VMEM((2, R, 6, *unit), jnp.bfloat16),
            pltpu.SemaphoreType.DMA((2,)),
            pltpu.SemaphoreType.DMA((2, R)),
            pltpu.SemaphoreType.DMA((2,)),
            pltpu.SemaphoreType.DMA((2, R, len(HOPS))),
            pltpu.SemaphoreType.DMA((X - 1,)),
            pltpu.SemaphoreType.DMA((X - 1,)),
        ],
        compiler_params=pltpu.CompilerParams(collective_id=0, has_side_effects=True, vmem_limit_bytes=50 << 20),
        name="exchange",
    )(table, land_values, area_weights, land_mask.reshape(blocks, 1, cells))
    near, far = near.reshape(planes * R, *unit), far.reshape(X - 1, planes * R, half, ROWS, tile_cells)
    return pl.pallas_call(
        functools.partial(place_kernel, pieces, planes),
        in_specs=[
            pl.BlockSpec(memory_space=pltpu.VMEM),
            pl.BlockSpec(memory_space=pltpu.VMEM),
            pl.BlockSpec(memory_space=pltpu.VMEM),
        ],
        out_specs=pl.BlockSpec(memory_space=pl.ANY),
        out_shape=jax.ShapeDtypeStruct((fields, tiles * tile_cells), jnp.float32),
        scratch_shapes=[
            pltpu.VMEM((fields, (tiles + 1) * tile_cells), jnp.float32),
            pltpu.VMEM((tiles, tile_cells), jnp.float32),
            pltpu.VMEM((8, 128), jnp.int32),
            pltpu.SMEM((8, 128), jnp.int32),
            pltpu.SMEM((X * CAP * planes * R + 8,), jnp.int32),
            pltpu.SemaphoreType.DMA,
            pltpu.SemaphoreType.DMA,
        ],
        compiler_params=pltpu.CompilerParams(vmem_limit_bytes=24 << 20),
        name="place",
    )(near.reshape(-1, ROWS, tile_cells), far.reshape(-1, ROWS, tile_cells), ocean_mask.reshape(tiles, tile_cells))


def solution(mesh):
    in_specs = (
        P(None, ("band", "sub")),
        P(("band", "sub"), None, None),
        P(("band", "sub")),
        P(("band", "sub"), None),
        P(("band", "sub")),
        P(("band", "sub")),
    )
    return jax.shard_map(
        per_device, mesh=mesh, in_specs=in_specs, out_specs=P(None, ("band", "sub")), check_vma=False
    )
```

time: 149 us -> 137 us (0.919)
  Pallas kernels: 147 us -> 137 us
  local copies, waits for them, and re-layouts: 2.23 us -> 0.01 us
    pallas_call x2, Pallas kernels: 24.5 us -> 9.27 us  [the longest x1 7.73 us: per_device(): pl.pallas_call(functools.partial(place_kernel, pieces, planes), in_specs=...]
    pallas_call x1, Pallas kernels: 123 us -> 127 us  [per_device(): pl.pallas_call(functools.partial(exchange_kernel, pieces), in_specs=[pl.B...]
    unnamed x4 -> x2, local copies, waits for them, and re-layouts: 2.23 us -> 0.01 us
where the time goes in v3:
time: 137 us
  Pallas kernels  137 us (100%)
    pallas_call x1, Pallas kernels, per_device(): pl.pallas_call(functools.partial(exchange_kernel, pieces), in_specs=[pl.B...  127 us
    pallas_call x1, Pallas kernels, per_device(): pl.pallas_call(functools.partial(place_kernel, pieces, planes), in_specs=...  7.73 us

profile of v3, /device:TPU:17, one launch (start us, length us, event | category | flops | bytes accessed | tf_op | source)
XLA Modules:
  0.0 136.6 jit_solution(13920631025758674433)
XLA Ops:
  0.0 0.0 copy-start
  0.0 1.5 %table.1.table_ref = s32[3,256]{1,0:T(4,128)} custom-call(s32[1,128]{1,0:T(1,128)} %bitcast.10, s32[1,128]{1,0:T(1,128)} %bitcast.11), custom_call_target="tpu_custom_call" | custom-call | tf_op jit(solution)/shard_map/table/pallas_call | solution.py:308
  1.5 127.3 %exchange.1 = (bf16[8,8,33,8,128]{4,3,2,1,0:T(8,128)(2,1)S(1)}, bf16[3,8,8,17,8,128]{5,4,3,2,1,0:T(8,128)(2,1)S(1)}) custom-call(s32[3,256]{1,0:T(4,128)} %table.1.table_ref, bf16[64,16384]{1,0:T(8,128)(2,1)} %values_hbm.1, bf16[128,128,128]{2,1,0:T(8,128)(2,1)} %weights_hbm.1, s32[128,1,128]{2,1,0:T(1,128)} %bitcast.9), custom_call_target="tpu_custom_call" | custom-call | tf_op jit(solution)/shard_map/exchange/pallas_call | solution.py:315
  128.9 0.0 copy-done
  128.9 7.7 %place.1 = f32[64,25600]{1,0:T(8,128)} custom-call(bf16[2112,8,128]{2,1,0:T(8,128)(2,1)S(1)} %bitcast.7, bf16[3264,8,128]{2,1,0:T(8,128)(2,1)S(1)} %bitcast.6, s32[200,128]{1,0:T(8,128)S(1)} %bitcast.8), custom_call_target="tpu_custom_call" | custom-call | tf_op jit(solution)/shard_map/place/pallas_call | solution.py:347
Async XLA Ops:
  0.0 128.9 %copy-start = (s32[25600]{0:T(1024)S(1)}, s32[25600]{0:T(1024)}, u32[]{:S(2)}) copy-start(s32[25600]{0:T(1024)} %param.11) | copy-start | bytes 307204

commit v4 on v3

--- a/solution.py
+++ b/solution.py
@@ -106,11 +106,7 @@
             fill(stage.at[i, ahead], ahead, to)
             return 0
 
-        if i == 0:
-            fill(near_ref.at[0, rem], 0, to)
-            lax.fori_loop(1, planes, one, 0)
-        else:
-            lax.fori_loop(0, planes, one, 0)
+        lax.fori_loop(1, planes, one, 0)
 
     right, left = (z + 1) % planes, (z + planes - 1) % planes
     ways = (1, X - 1, 2)
@@ -122,8 +118,10 @@
         pl.semaphore_signal(barrier, inc=1, device_id=peer, device_id_type=MESH)
     for load in loads:
         load.wait()
+    fill(near_ref.at[0, rem], 0, rem)
+    for i in range(1, R):
+        fill(stage.at[i, 0], 0, mate(i, 1))
     prepare(0)
-    prepare(1)
     pl.semaphore_wait(barrier, len(greeted))
 
     def remote(src, dst, send_sem, recv_sem, peer):
@@ -135,11 +133,7 @@
         to = mate(i, 1)
         src = stage.at[i, pl.ds(1, planes - 1)] if onward else stage.at[i, 0]
         dst = held.at[:, rem] if onward else near_ref.at[0, rem]
-        return remote(src, dst, y_send.at[onward], y_recv.at[onward, i], device(rem_to=to))
-
-    def y_start(i):
-        for onward in (1, 0):
-            y_copy(i, onward).start()
+        return remote(src, dst, y_send.at[onward, i], y_recv.at[onward, i], device(rem_to=to))
 
     def forward(ahead, source):
         for way, shift in enumerate(ways):
@@ -172,8 +166,25 @@
         else:
             z_copy(i, way, far, hop + 1).start()
 
-    prepared = 1
+    def own_plane(i):
+        y_copy(i, 0).wait_recv()
+        forward(0, mate(i, -1))
+
+    computed = {0: (2, 1, 3), 1: (4, 5), 3: (6, 7)}
+    sent = {0: (2, 1, 3), 2: (4, 5), 4: (6,), 5: (7,)}
+
+    def arrivals(turn):
+        for hop in (1, 2, 3, 4):
+            i = turn - hop
+            if 0 <= i < R:
+                for far in range(hop, 5):
+                    for way in (0, 1):
+                        if travels(i, way, far):
+                            arrive(i, way, far, hop)
+
     for turn in range(R + 4):
+        if turn == 2:
+            arrivals(turn)
         if turn < R:
             if turn > 0:
                 y_copy(turn, 1).wait_recv()
@@ -181,25 +192,28 @@
                 for way in (0, 1):
                     if travels(turn, way, far):
                         z_copy(turn, way, far, 1).start()
-            if turn > 0:
-                y_copy(turn, 0).wait_recv()
-            forward(0, mate(turn, -1))
-        for _ in range(2 if turn < 2 else 1):
-            if prepared < R:
-                if prepared + 1 < R:
-                    prepare(prepared + 1)
-                y_start(prepared)
-                prepared += 1
-        for hop in (1, 2, 3, 4):
-            i = turn - hop
-            if 0 <= i < R:
-                for far in range(hop, 5):
-                    for way in (0, 1):
-                        if travels(i, way, far):
-                            arrive(i, way, far, hop)
-
-    remote(near_ref.at[0, pl.ds(0, R - 1)], near_ref.at[0, pl.ds(0, R - 1)], y_send.at[0], y_recv.at[0, 0], device()).wait_send()
-    remote(held.at[:, pl.ds(0, R - 1)], held.at[:, pl.ds(0, R - 1)], y_send.at[1], y_recv.at[0, 0], device()).wait_send()
+        if turn == 0:
+            for i in range(1, R):
+                y_copy(i, 0).start()
+            forward(0, rem)
+        if turn == 1:
+            for i in range(1, R):
+                own_plane(i)
+        for i in computed.get(turn, ()):
+            prepare(i)
+            if i in sent.get(turn, ()):
+                y_copy(i, 1).start()
+        for i in sent.get(turn, ()):
+            if i not in computed.get(turn, ()):
+                y_copy(i - 2, 1).wait_send()
+                y_copy(i, 1).start()
+        if turn != 2:
+            arrivals(turn)
+
+    for i in range(1, R):
+        y_copy(i, 0).wait_send()
+        if i not in (2, 3, 4, 5):
+            y_copy(i, 1).wait_send()
     for way in (0, 1):
         remote(near_ref, near_ref, z_send.at[way], y_recv.at[0, 0], device()).wait_send()
     for way in range(X - 1):
@@ -333,7 +347,7 @@
             pltpu.VMEM((R, planes, *unit), jnp.bfloat16),
             pltpu.VMEM((planes - 1, R, *unit), jnp.bfloat16),
             pltpu.VMEM((2, R, 6, *unit), jnp.bfloat16),
-            pltpu.SemaphoreType.DMA((2,)),
+            pltpu.SemaphoreType.DMA((2, R)),
             pltpu.SemaphoreType.DMA((2, R)),
             pltpu.SemaphoreType.DMA((2,)),
             pltpu.SemaphoreType.DMA((2, R, len(HOPS))),

time: 137 us -> 131 us (0.956)
  the two profiles are of different devices: /device:TPU:17 before, /device:TPU:1 now
where the time goes in v4:
time: 131 us
  Pallas kernels  131 us (100%)
    pallas_call x1, Pallas kernels, per_device(): pl.pallas_call(functools.partial(exchange_kernel, pieces), in_specs=[pl.B...  122 us
    pallas_call x1, Pallas kernels, per_device(): pl.pallas_call(functools.partial(place_kernel, pieces, planes), in_specs=...  7.61 us

profile of v4, /device:TPU:1, one launch (start us, length us, event | category | flops | bytes accessed | tf_op | source)
XLA Modules:
  0.0 131.2 jit_solution(3316756964958276104)
XLA Ops:
  0.0 0.0 copy-start
  0.0 1.5 %table.1.table_ref = s32[3,256]{1,0:T(4,128)} custom-call(s32[1,128]{1,0:T(1,128)} %bitcast.10, s32[1,128]{1,0:T(1,128)} %bitcast.11), custom_call_target="tpu_custom_call" | custom-call | tf_op jit(solution)/shard_map/table/pallas_call | solution.py:322
  1.5 122.0 %exchange.1 = (bf16[8,8,33,8,128]{4,3,2,1,0:T(8,128)(2,1)S(1)}, bf16[3,8,8,17,8,128]{5,4,3,2,1,0:T(8,128)(2,1)S(1)}) custom-call(s32[3,256]{1,0:T(4,128)} %table.1.table_ref, bf16[64,16384]{1,0:T(8,128)(2,1)} %values_hbm.1, bf16[128,128,128]{2,1,0:T(8,128)(2,1)} %weights_hbm.1, s32[128,1,128]{2,1,0:T(1,128)} %bitcast.9), custom_call_target="tpu_custom_call" | custom-call | tf_op jit(solution)/shard_map/exchange/pallas_call | solution.py:329
  123.5 0.0 copy-done
  123.6 7.6 %place.1 = f32[64,25600]{1,0:T(8,128)} custom-call(bf16[2112,8,128]{2,1,0:T(8,128)(2,1)S(1)} %bitcast.7, bf16[3264,8,128]{2,1,0:T(8,128)(2,1)S(1)} %bitcast.6, s32[200,128]{1,0:T(8,128)S(1)} %bitcast.8), custom_call_target="tpu_custom_call" | custom-call | tf_op jit(solution)/shard_map/place/pallas_call | solution.py:361
Async XLA Ops:
  0.0 123.5 %copy-start = (s32[25600]{0:T(1024)S(1)}, s32[25600]{0:T(1024)}, u32[]{:S(2)}) copy-start(s32[25600]{0:T(1024)} %param.11) | copy-start | bytes 307204

commit v5 on v4

--- a/solution.py
+++ b/solution.py
@@ -23,10 +23,11 @@
     return z, x_lo, rem, sub * XLO + x_lo
 
 
-def table_kernel(band_ref, tile_ref, out_ref):
+def make_table(band_ref, tile_ref, out_ref):
     blocks = band_ref.shape[1]
     down = lax.broadcasted_iota(jnp.int32, (blocks, blocks), 0)
     across = lax.broadcasted_iota(jnp.int32, (blocks, blocks), 1)
+    out_ref[...] = jnp.zeros_like(out_ref)
     band = jnp.broadcast_to(band_ref[...], (blocks, blocks))
     tile = jnp.broadcast_to(tile_ref[...], (blocks, blocks))
     band_down = jnp.sum(jnp.where(down == across, band, 0), axis=1, keepdims=True)
@@ -46,14 +47,18 @@
 
 
 def exchange_kernel(
-    pieces, table_ref, values_hbm, weights_hbm, mask_hbm, near_ref, far_ref,
-    values_ref, weights_ref, mask_ref, in_sem, stage, held, relay, y_send, y_recv, z_send, z_recv, x_send, x_recv,
+    pieces, band_hbm, tile_hbm, values_hbm, weights_hbm, mask_hbm, near_ref, far_ref,
+    band_ref, tile_ref, table_vmem, table_ref, values_ref, weights_ref, mask_ref, in_sem, stage, held, relay, y_send, y_recv, z_send, z_recv, x_send, x_recv,
 ):
+    names = [
+        pltpu.make_async_copy(band_hbm, band_ref, in_sem.at[3]),
+        pltpu.make_async_copy(tile_hbm, tile_ref, in_sem.at[4]),
+    ]
     loads = [
         pltpu.make_async_copy(weights_hbm, weights_ref, in_sem.at[1]),
         pltpu.make_async_copy(mask_hbm, mask_ref, in_sem.at[2]),
     ]
-    for load in loads:
+    for load in names + loads:
         load.start()
 
     def load_block(block, _):
@@ -116,6 +121,11 @@
     greeted += [device(x_to=(x + shift) % X) for shift in ways]
     for peer in greeted:
         pl.semaphore_signal(barrier, inc=1, device_id=peer, device_id_type=MESH)
+    for load in names:
+        load.wait()
+    make_table(band_ref, tile_ref, table_vmem)
+    loads.append(pltpu.make_async_copy(table_vmem, table_ref, in_sem.at[5]))
+    loads[-1].start()
     for load in loads:
         load.wait()
     fill(near_ref.at[0, rem], 0, rem)
@@ -319,31 +329,23 @@
     half = CAP * pieces + 1
     tiles = ocean_mask.shape[0] // tile_cells
     unit = (2 * half - 1, ROWS, tile_cells)
-    table = pl.pallas_call(
-        table_kernel,
-        in_specs=[pl.BlockSpec(memory_space=pltpu.VMEM)] * 2,
-        out_specs=pl.BlockSpec(memory_space=pltpu.VMEM),
-        out_shape=jax.ShapeDtypeStruct((3, bands * CAP), jnp.int32),
-        name="table",
-    )(dest_band.reshape(1, blocks), dest_tile.reshape(1, blocks))
     near, far = pl.pallas_call(
         functools.partial(exchange_kernel, pieces),
-        in_specs=[
-            pl.BlockSpec(memory_space=pltpu.SMEM),
-            pl.BlockSpec(memory_space=pltpu.HBM),
-            pl.BlockSpec(memory_space=pltpu.HBM),
-            pl.BlockSpec(memory_space=pltpu.HBM),
-        ],
+        in_specs=[pl.BlockSpec(memory_space=pltpu.HBM)] * 5,
         out_specs=[pl.BlockSpec(memory_space=pltpu.VMEM)] * 2,
         out_shape=[
             pltpu.VMEM((planes, R, *unit), jnp.bfloat16),
             pltpu.VMEM((X - 1, planes, R, half, ROWS, tile_cells), jnp.bfloat16),
         ],
         scratch_shapes=[
+            pltpu.VMEM((1, blocks), jnp.int32),
+            pltpu.VMEM((1, blocks), jnp.int32),
+            pltpu.VMEM((8, bands * CAP), jnp.int32),
+            pltpu.SMEM((8, bands * CAP), jnp.int32),
             pltpu.VMEM((blocks, fields, cells), jnp.bfloat16),
             pltpu.VMEM(area_weights.shape, jnp.bfloat16),
             pltpu.VMEM((blocks, 1, cells), jnp.int32),
-            pltpu.SemaphoreType.DMA((3,)),
+            pltpu.SemaphoreType.DMA((6,)),
             pltpu.VMEM((R, planes, *unit), jnp.bfloat16),
             pltpu.VMEM((planes - 1, R, *unit), jnp.bfloat16),
             pltpu.VMEM((2, R, 6, *unit), jnp.bfloat16),
@@ -356,7 +358,13 @@
         ],
         compiler_params=pltpu.CompilerParams(collective_id=0, has_side_effects=True, vmem_limit_bytes=50 << 20),
         name="exchange",
-    )(table, land_values, area_weights, land_mask.reshape(blocks, 1, cells))
+    )(
+        dest_band.reshape(1, blocks),
+        dest_tile.reshape(1, blocks),
+        land_values,
+        area_weights,
+        land_mask.reshape(blocks, 1, cells),
+    )
     near, far = near.reshape(planes * R, *unit), far.reshape(X - 1, planes * R, half, ROWS, tile_cells)
     return pl.pallas_call(
         functools.partial(place_kernel, pieces, planes),

time: 131 us -> 129 us (0.985)
  Pallas kernels: 131 us -> 129 us
    pallas_call x1 -> x0, Pallas kernels: 1.54 us -> none  [per_device(): pl.pallas_call(table_kernel, in_specs=[pl.BlockSpec(memory_space=pltpu.VM...]
where the time goes in v5:
time: 129 us
  Pallas kernels  129 us (100%)
    pallas_call x1, Pallas kernels, per_device(): pl.pallas_call(functools.partial(exchange_kernel, pieces), in_specs=[pl.B...  121 us
    pallas_call x1, Pallas kernels, per_device(): pl.pallas_call(functools.partial(place_kernel, pieces, planes), in_specs=...  7.65 us

profile of v5, /device:TPU:1, one launch (start us, length us, event | category | flops | bytes accessed | tf_op | source)
XLA Modules:
  0.0 129.1 jit_solution(18244734268958251391)
XLA Ops:
  0.0 0.0 copy-start
  0.0 121.4 %exchange.1 = (bf16[8,8,33,8,128]{4,3,2,1,0:T(8,128)(2,1)S(1)}, bf16[3,8,8,17,8,128]{5,4,3,2,1,0:T(8,128)(2,1)S(1)}) custom-call(s32[1,128]{1,0:T(1,128)} %bitcast.10, s32[1,128]{1,0:T(1,128)} %bitcast.11, bf16[64,16384]{1,0:T(8,128)(2,1)} %values_hbm.1, bf16[128,128,128]{2,1,0:T(8,128)(2,1)} %weights_hbm.1, s32[128,1,128]{2,1,0:T(1,128)} %bitcast.9), custom_call_target="tpu_custom_call" | custom-call | tf_op jit(solution)/shard_map/exchange/pallas_call | solution.py:332
  121.4 0.0 copy-done
  121.4 7.7 %place.1 = f32[64,25600]{1,0:T(8,128)} custom-call(bf16[2112,8,128]{2,1,0:T(8,128)(2,1)S(1)} %bitcast.7, bf16[3264,8,128]{2,1,0:T(8,128)(2,1)S(1)} %bitcast.6, s32[200,128]{1,0:T(8,128)S(1)} %bitcast.8), custom_call_target="tpu_custom_call" | custom-call | tf_op jit(solution)/shard_map/place/pallas_call | solution.py:369
Async XLA Ops:
  0.0 121.4 %copy-start = (s32[25600]{0:T(1024)S(1)}, s32[25600]{0:T(1024)}, u32[]{:S(2)}) copy-start(s32[25600]{0:T(1024)} %param.11) | copy-start | bytes 307204
